TPU v7x, 256 devices: a whole 4x4x8 slice. The times are simulated.
256 devices in a mesh: items: 4 (over x), users: 64 (over z, y, core).
Axes of the slice: x: 4, y: 4, z: 8, core: 2. Of those that a mesh axis runs over, the one named last changes fastest.
Arguments:
- capsules: bfloat16 [4096, 8, 128], P('users'), may hold values from -6 to 6
- bank: bfloat16 [262144, 128], P(('items', 'users')), may hold values from -0.5 to 0.5
Outputs:
- relative: float32 [4096, 256], P('users', 'items')
- peak: float32 [4096], P('users')
All inputs are finite; a program needn't handle non-finite values.
Results may differ from a plain program's by a relative error of at most 0.0003.
Values may be sent and summed in bfloat16 or wider, within the bound.
A program may use at most 64 MiB of HBM per device.

v0:
```python
import jax
import jax.numpy as jnp
from jax import lax
from jax.sharding import PartitionSpec as P

BLOCK = 1024


def sent_to_all(value, axis):
    length = lax.axis_size(axis)
    return lax.all_to_all(
        jnp.broadcast_to(value[None], (length, *value.shape)), axis, 0, 0, tiled=True
    )


def of_everyone(value, axis):
    return sent_to_all(value, axis).max(axis=0)


def block_peaks(caps, rows):
    users_here = caps.shape[0]
    flat = caps.reshape(users_here * caps.shape[1], caps.shape[2])
    count = rows.shape[0] // BLOCK
    blocks = rows.reshape(count, BLOCK, rows.shape[1])

    def one_block(item_rows):
        score = lax.dot_general(
            flat, item_rows, (((1,), (1,)), ((), ())), preferred_element_type=jnp.float32
        )
        return jnp.max(score.reshape(users_here, -1), axis=1)

    return lax.map(one_block, blocks).T


def per_device(capsules, bank):
    everyone = lax.all_gather(capsules, "users", axis=0, tiled=True)
    own_block = block_peaks(everyone, bank)
    table = lax.all_to_all(own_block, "users", split_axis=0, concat_axis=1, tiled=True)
    peak = of_everyone(jnp.max(table, axis=1), "items")
    return (table - peak[:, None], peak)


def solution(mesh):
    return jax.shard_map(
        per_device,
        mesh=mesh,
        in_specs=(P("users", None, None), P(("items", "users"), None)),
        out_specs=(P("users", "items"), P("users")),
        check_vma=False,
    )
```

profile of v0, /device:TPU:1, one launch (start us, length us, event | category | flops | bytes accessed | tf_op | source)
XLA Modules:
  0.0 152.0 jit_solution(13896020500113062206)
XLA Ops:
  7.2 0.0 copy-start
  7.2 0.0 all-gather.2.cloned.1.call-start
  7.2 0.7 all-gather.2.cloned.1.call-update
  7.9 90.1 %all-gather.2.cloned.1.call-done = bf16[4096,8,128]{2,1,0:T(8,128)(2,1)} async-done(((bf16[64,8,128]{2,1,0:T(8,128)(2,1)}), bf16[4096,8,128]{2,1,0:T(8,128)(2,1)}) %all-gather.2.cloned.1.call-update) | async-done | bytes 8388624 | tf_op jit(solution)/shard_map/all_gather | solution.py:36
  98.0 0.0 copy-done
  98.0 21.6 %convolution_reduce_fusion = f32[32768]{0:T(1024)S(1)} fusion(bf16[1024,128]{1,0:T(8,128)(2,1)S(1)} %copy-done, bf16[4096,8,128]{2,1,0:T(8,128)(2,1)} %all-gather.2.cloned.1.call-done), kind=kOutput, calls=%fused_computation | convolution fusion | flops 8623456256 | bytes 8781824 | tf_op jit(solution)/shard_map/while/body/eval_jaxpr/dot_general | solution.py:27
  119.6 1.1 reduce_max.36
  120.7 0.6 reduce_max.37
  121.3 0.1 all_to_all.18
  121.4 15.0 %all_to_all.25 = f32[64,64,1]{1,2,0:T(1,128)S(1)} all-to-all(f32[64,64,1]{1,2,0:T(1,128)S(1)} %bitcast.10), channel_id=1, replica_groups=mesh['items'=4,'users'=64] {'users'}, dimensions={0} | all-to-all | bytes 32768 | tf_op jit(solution)/shard_map/all_to_all | solution.py:38
  136.4 0.1 reduce_max.38
  136.5 7.9 %all_to_all.26 = f32[4,1,64]{2,1,0:T(1,128)S(1)} all-to-all(f32[4,1,64]{2,1,0:T(1,128)S(1)} %broadcast_in_dim.5), channel_id=1, replica_groups=mesh['items'=4,'users'=64] {'items'}, dimensions={0} | all-to-all | bytes 2048 | tf_op jit(solution)/shard_map/all_to_all | solution.py:11
  144.4 0.0 copy-start.1
  144.4 0.7 copy.11
  145.1 0.0 copy-done.1
  (3 shorter events, 0.0 us)
Async XLA Ops:
  7.2 90.8 %copy-start = (bf16[1024,128]{1,0:T(8,128)(2,1)S(1)}, bf16[1024,128]{1,0:T(8,128)(2,1)}, u32[]{:S(2)}) copy-start(bf16[1024,128]{1,0:T(8,128)(2,1)} %param.3) | copy-start | bytes 786436
  7.2 90.8 %all-gather.2.cloned.1.call-start = ((), (), s32[]{:S(2)}) async-start(), calls=%async_computation.2 | async-start | bytes 8519680 | tf_op jit(solution)/shard_map/all_gather | solution.py:36
  144.4 0.7 copy-start.1
Sparse Core Ops, SparseCore 0:
  10.8 87.1 all-gather.1
where the time goes:
time: 152 us
  waiting for transfers between devices  90.8 us (60%)
  blocking collectives  22.9 us (15%)
  matrix products  21.6 us (14%)
  between operations  14.1 us (9%)
  local copies, waits for them, and re-layouts  1.92 us (1%)
    all_gather x1, waiting for transfers between devices, per_device(): everyone = lax.all_gather(capsules, 'users', axis=0, tiled=True)  90.1 us
    dot_general x1, matrix products, one_block(): lax.dot_general(flat, item_rows, (((1,), (1,)), ((), ())), preferred_elem...  21.6 us
    all_to_all x1, blocking collectives, per_device(): lax.all_to_all(own_block, 'users', split_axis=0, concat_axis=1, tiled=True)  15 us
    all_to_all x1, blocking collectives, sent_to_all(): lax.all_to_all(jnp.broadcast_to(value[None], (length, *value.shape)), axi...  7.9 us
  transfers between devices with their start and end apart: 1, of which 1 were waited for; matrix products, arithmetic and copies ran while one was open for 0% of the time, Pallas kernels for 0%

commit v1 on v0

--- a/solution.py
+++ b/solution.py
@@ -35,7 +35,12 @@
 def per_device(capsules, bank):
     everyone = lax.all_gather(capsules, "users", axis=0, tiled=True)
     own_block = block_peaks(everyone, bank)
-    table = lax.all_to_all(own_block, "users", split_axis=0, concat_axis=1, tiled=True)
+    table = jnp.concatenate(
+        lax.all_to_all(
+            jnp.stack(jnp.split(own_block, lax.axis_size("users"), axis=0)), "users", 0, 0
+        ),
+        axis=1,
+    )
     peak = of_everyone(jnp.max(table, axis=1), "items")
     return (table - peak[:, None], peak)
 

time: 152 us -> 155 us (1.020)
  local copies, waits for them, and re-layouts: 1.92 us -> 4.61 us
    unnamed x5 -> x68, local copies, waits for them, and re-layouts: 0.71 us -> 3.4 us
where the time goes in v1:
time: 155 us
  waiting for transfers between devices  90.8 us (59%)
  blocking collectives  22.9 us (15%)
  matrix products  21.6 us (14%)
  between operations  14.1 us (9%)
  local copies, waits for them, and re-layouts  4.61 us (3%)
    all_gather x1, waiting for transfers between devices, per_device(): everyone = lax.all_gather(capsules, 'users', axis=0, tiled=True)  90.1 us
    dot_general x1, matrix products, one_block(): lax.dot_general(flat, item_rows, (((1,), (1,)), ((), ())), preferred_elem...  21.6 us
    all_to_all x1, blocking collectives, per_device(): lax.all_to_all(jnp.stack(jnp.split(own_block, lax.axis_size('users'), axi...  15 us
    all_to_all x1, blocking collectives, sent_to_all(): lax.all_to_all(jnp.broadcast_to(value[None], (length, *value.shape)), axi...  7.9 us
    unnamed x68, local copies, waits for them, and re-layouts  3.4 us
  transfers between devices with their start and end apart: 1, of which 1 were waited for; matrix products, arithmetic and copies ran while one was open for 0% of the time, Pallas kernels for 0%

profile of v1, /device:TPU:1, one launch (start us, length us, event | category | flops | bytes accessed | tf_op | source)
XLA Modules:
  0.0 154.7 jit_solution(17348725484174725983)
XLA Ops:
  7.2 0.0 copy-start
  7.2 0.0 all-gather.2.cloned.1.call-start
  7.2 0.7 all-gather.2.cloned.1.call-update
  7.9 90.1 %all-gather.2.cloned.1.call-done = bf16[4096,8,128]{2,1,0:T(8,128)(2,1)} async-done(((bf16[64,8,128]{2,1,0:T(8,128)(2,1)}), bf16[4096,8,128]{2,1,0:T(8,128)(2,1)}) %all-gather.2.cloned.1.call-update) | async-done | bytes 8388624 | tf_op jit(solution)/shard_map/all_gather | solution.py:36
  98.0 0.0 copy-done
  98.0 21.6 %convolution_reduce_fusion = f32[32768]{0:T(1024)S(1)} fusion(bf16[1024,128]{1,0:T(8,128)(2,1)S(1)} %copy-done, bf16[4096,8,128]{2,1,0:T(8,128)(2,1)} %all-gather.2.cloned.1.call-done), kind=kOutput, calls=%fused_computation | convolution fusion | flops 8623456256 | bytes 8781824 | tf_op jit(solution)/shard_map/while/body/eval_jaxpr/dot_general | solution.py:27
  119.6 1.1 reduce_max.36
  120.7 0.6 reduce_max.37
  121.4 0.1 constant_dynamic-update-slice_fusion.62
  121.4 0.1 constant_dynamic-update-slice_fusion.60
  121.5 0.1 constant_dynamic-update-slice_fusion.58
  121.6 0.1 constant_dynamic-update-slice_fusion.56
  121.7 0.1 constant_dynamic-update-slice_fusion.54
  121.8 0.1 constant_dynamic-update-slice_fusion.52
  121.9 0.1 constant_dynamic-update-slice_fusion.50
  122.0 0.1 constant_dynamic-update-slice_fusion.48
  122.1 0.1 constant_dynamic-update-slice_fusion.46
  122.1 0.1 constant_dynamic-update-slice_fusion.44
  122.2 0.1 constant_dynamic-update-slice_fusion.42
  122.3 0.1 constant_dynamic-update-slice_fusion.40
  122.4 0.1 constant_dynamic-update-slice_fusion.38
  122.5 0.1 constant_dynamic-update-slice_fusion.36
  122.6 0.1 constant_dynamic-update-slice_fusion.34
  122.7 0.1 constant_dynamic-update-slice_fusion.32
  122.8 0.1 constant_dynamic-update-slice_fusion.30
  122.8 0.1 constant_dynamic-update-slice_fusion.28
  122.9 0.1 constant_dynamic-update-slice_fusion.26
  123.0 0.1 constant_dynamic-update-slice_fusion.24
  123.1 0.1 constant_dynamic-update-slice_fusion.22
  123.2 0.1 constant_dynamic-update-slice_fusion.20
  123.3 0.1 constant_dynamic-update-slice_fusion.18
  123.4 0.1 constant_dynamic-update-slice_fusion.16
  123.5 0.1 constant_dynamic-update-slice_fusion.14
  123.5 0.1 constant_dynamic-update-slice_fusion.12
  123.6 0.1 constant_dynamic-update-slice_fusion.10
  123.7 0.1 constant_dynamic-update-slice_fusion.8
  123.8 0.1 constant_dynamic-update-slice_fusion.6
  123.9 0.1 constant_dynamic-update-slice_fusion.4
  124.0 0.1 constant_dynamic-update-slice_fusion.2
  124.1 0.1 constant_dynamic-update-slice_fusion
  124.1 15.0 %all_to_all.11 = f32[64,64,1]{1,2,0:T(1,128)S(1)} all-to-all(f32[64,64,1]{1,2,0:T(1,128)S(1)} %constant_dynamic-update-slice_fusion), channel_id=1, replica_groups=mesh['items'=4,'users'=64] {'users'}, dimensions={0} | all-to-all | bytes 32768 | tf_op jit(solution)/shard_map/all_to_all | solution.py:39
  139.1 0.1 reduce_max.38
  139.2 7.9 %all_to_all.12 = f32[4,1,64]{2,1,0:T(1,128)S(1)} all-to-all(f32[4,1,64]{2,1,0:T(1,128)S(1)} %broadcast_in_dim.5), channel_id=1, replica_groups=mesh['items'=4,'users'=64] {'items'}, dimensions={0} | all-to-all | bytes 2048 | tf_op jit(solution)/shard_map/all_to_all | solution.py:11
  147.1 0.0 copy-start.1
  147.1 0.7 copy.9
  147.8 0.0 copy-done.1
  (35 shorter events, 0.3 us)
Async XLA Ops:
  7.2 90.8 %copy-start = (bf16[1024,128]{1,0:T(8,128)(2,1)S(1)}, bf16[1024,128]{1,0:T(8,128)(2,1)}, u32[]{:S(2)}) copy-start(bf16[1024,128]{1,0:T(8,128)(2,1)} %param.3) | copy-start | bytes 786436
  7.2 90.8 %all-gather.2.cloned.1.call-start = ((), (), s32[]{:S(2)}) async-start(), calls=%async_computation.2 | async-start | bytes 8519680 | tf_op jit(solution)/shard_map/all_gather | solution.py:36
  147.1 0.7 copy-start.1
Sparse Core Ops, SparseCore 0:
  10.8 87.1 all-gather.1

commit v2 on v0

--- a/solution.py
+++ b/solution.py
@@ -33,7 +33,9 @@
 
 
 def per_device(capsules, bank):
-    everyone = lax.all_gather(capsules, "users", axis=0, tiled=True)
+    everyone = jnp.concatenate(
+        lax.all_to_all(jnp.stack([capsules] * lax.axis_size("users")), "users", 0, 0), axis=0
+    )
     own_block = block_peaks(everyone, bank)
     table = lax.all_to_all(own_block, "users", split_axis=0, concat_axis=1, tiled=True)
     peak = of_everyone(jnp.max(table, axis=1), "items")

time: 152 us -> 246 us (1.62)
  blocking collectives: 22.9 us -> 222 us
  waiting for transfers between devices: 90.8 us -> 0 us
  between operations: 14.1 us -> 0.68 us
  matrix products: 21.6 us -> 18.2 us
  local copies, waits for them, and re-layouts: 1.92 us -> 4.87 us
    all_to_all x0 -> x1, blocking collectives: none -> 197 us  [per_device(): lax.all_to_all(jnp.stack([capsules] * lax.axis_size('users')), 'users', 0...]
    all_gather x1 -> x0, waiting for transfers between devices: 90.1 us -> none  [per_device(): everyone = lax.all_gather(capsules, 'users', axis=0, tiled=True)]
    dot_general x1, matrix products: 21.6 us -> 18.2 us  [one_block(): lax.dot_general(flat, item_rows, (((1,), (1,)), ((), ())), preferred_elem...]
    another operation x0 -> x1, local copies, waits for them, and re-layouts: none -> 2.96 us  [per_device(): jnp.stack([capsules] * lax.axis_size('users'))]
  transfers between devices with their start and end apart: 1 -> 0, of which waited for: 1 -> 0; matrix products, arithmetic and copies ran while one was open for 0% -> 0% of each run, Pallas kernels for 0% -> 0%
where the time goes in v2:
time: 246 us
  blocking collectives  222 us (90%)
  matrix products  18.2 us (7%)
  local copies, waits for them, and re-layouts  4.87 us (2%)
    all_to_all x1, blocking collectives, per_device(): lax.all_to_all(jnp.stack([capsules] * lax.axis_size('users')), 'users', 0...  197 us
    dot_general x1, matrix products, one_block(): lax.dot_general(flat, item_rows, (((1,), (1,)), ((), ())), preferred_elem...  18.2 us
    all_to_all x1, blocking collectives, per_device(): lax.all_to_all(own_block, 'users', split_axis=0, concat_axis=1, tiled=True)  16.2 us
    all_to_all x1, blocking collectives, sent_to_all(): lax.all_to_all(jnp.broadcast_to(value[None], (length, *value.shape)), axi...  7.94 us

profile of v2, /device:TPU:1, one launch (start us, length us, event | category | flops | bytes accessed | tf_op | source)
XLA Modules:
  0.0 246.1 jit_solution(8156816575158829962)
XLA Ops:
  0.6 0.0 copy-start
  0.6 3.0 %stack.2 = bf16[64,64,8,128]{3,2,1,0:T(8,128)(2,1)S(1)} broadcast(bf16[64,8,128]{2,1,0:T(8,128)(2,1)} %param.2), dimensions={1,2,3} | broadcast | bytes 8519680 | tf_op jit(solution)/shard_map/stack | solution.py:37
  3.6 197.5 %all_to_all.30 = bf16[64,64,8,128]{3,2,1,0:T(8,128)(2,1)S(1)} all-to-all(bf16[64,64,8,128]{3,2,1,0:T(8,128)(2,1)S(1)} %stack.2), channel_id=1, replica_groups=mesh['items'=4,'users'=64] {'users'}, dimensions={0} | all-to-all | bytes 16777216 | tf_op jit(solution)/shard_map/all_to_all | solution.py:37
  201.1 0.0 copy-done
  201.1 18.2 %convolution_reduce_fusion = f32[32768]{0:T(1024)S(1)} fusion(bf16[32768,128]{1,0:T(8,128)(2,1)S(1)} %bitcast.8, bf16[1024,128]{1,0:T(8,128)(2,1)S(1)} %copy-done), kind=kOutput, calls=%fused_computation | convolution fusion | flops 8623456256 | bytes 8781824 | tf_op jit(solution)/shard_map/while/body/eval_jaxpr/dot_general | solution.py:27
  219.3 1.1 reduce_max.36
  220.5 0.6 reduce_max.37
  221.1 0.1 all_to_all.22
  221.2 16.2 %all_to_all.31 = f32[64,64,1]{1,2,0:T(1,128)S(1)} all-to-all(f32[64,64,1]{1,2,0:T(1,128)S(1)} %bitcast.10), channel_id=1, replica_groups=mesh['items'=4,'users'=64] {'users'}, dimensions={0} | all-to-all | bytes 32768 | tf_op jit(solution)/shard_map/all_to_all | solution.py:40
  237.3 0.1 reduce_max.38
  237.4 7.9 %all_to_all.32 = f32[4,1,64]{2,1,0:T(1,128)S(1)} all-to-all(f32[4,1,64]{2,1,0:T(1,128)S(1)} %broadcast_in_dim.5), channel_id=1, replica_groups=mesh['items'=4,'users'=64] {'items'}, dimensions={0} | all-to-all | bytes 2048 | tf_op jit(solution)/shard_map/all_to_all | solution.py:11
  245.4 0.0 copy-start.1
  245.4 0.7 copy.11
  246.1 0.0 copy-done.1
  (3 shorter events, 0.0 us)
Async XLA Ops:
  0.6 200.5 %copy-start = (bf16[1024,128]{1,0:T(8,128)(2,1)S(1)}, bf16[1024,128]{1,0:T(8,128)(2,1)}, u32[]{:S(2)}) copy-start(bf16[1024,128]{1,0:T(8,128)(2,1)} %param.3) | copy-start | bytes 786436
  245.4 0.7 copy-start.1
